TPU v7x, 768 devices: a whole 4x8x12 slice. The times are simulated.
768 devices in a mesh: dp: 192 (over y, z, core), sp: 4 (over x).
Axes of the slice: x: 4, y: 8, z: 12, core: 2. Of those that a mesh axis runs over, the one named last changes fastest.
Arguments:
- hidden: bfloat16 [192, 4, 128, 3584], P('dp', None, 'sp'), may hold values from -6 to 6
- segment_ids: int32 [192, 4, 128], P('dp'), may hold values from -1 to 15, as said below
- w_query: bfloat16 [3584, 3584], P(None, 'sp'), may hold values from -0.10022297 to 0.10022297
- key_matrix: bfloat16 [3584, 512], P(None, 'sp'), may hold values from -0.10022297 to 0.10022297
- value_matrix: bfloat16 [3584, 512], P(None, 'sp'), may hold values from -0.10022297 to 0.10022297
Outputs:
- mixed: bfloat16 [192, 512, 3584], P('dp', 'sp')
Inputs may be any that keep to these rules, and one draw needn't show every extreme that they name: `segment_ids`: in each outbox the live slots come first; over them the ids start at 0 and never fall, by steps of 0 or 1; empty slots hold -1. Every group has an outbox whose 128 slots are all live.
All inputs are finite; a program needn't handle non-finite values.
Results may differ from a plain program's by a relative error of at most 0.0087.
Values may be sent and summed in bfloat16 or wider, within the bound.
A program may use at most 64 MiB of HBM per device.

v0:
```python
import jax
import jax.numpy as jnp
from jax import lax
from jax.sharding import PartitionSpec as P

HEAD_SIZE = 128
NSEG = 16
GROUP_SLOTS = 512


ROPE_BASE = 1000000.0


def shifted(value, axis, steps):
    count = lax.axis_size(axis)
    pairs = [(source, (source + steps) % count) for source in range(count)]
    return lax.ppermute(value, axis, pairs)


def rotate(tensor, where):
    half_width = tensor.shape[-1] // 2
    freq = ROPE_BASE ** (-(jnp.arange(half_width, dtype=jnp.float32) * 2.0 / tensor.shape[-1]))
    angle = where[:, None] * freq[None, :]
    cosine = jnp.cos(angle)[:, None, :]
    sine = jnp.sin(angle)[:, None, :]
    first = tensor[..., :half_width]
    second = tensor[..., half_width:]
    return jnp.concatenate(
        [first * cosine - second * sine, second * cosine + first * sine], axis=-1
    )


def positions(segments):
    slot_ids = jnp.arange(NSEG, dtype=jnp.int32)
    onehot = (segments[..., :, None] == slot_ids).astype(jnp.int32)
    living = (segments >= 0).astype(jnp.int32)
    below = jnp.sum(
        (segments[..., :, None] < slot_ids).astype(jnp.int32) * living[..., :, None], axis=-2
    )
    first_slot = jnp.sum(onehot * below[..., None, :], axis=-1)
    index = jnp.arange(segments.shape[-1], dtype=jnp.int32)
    return (index - first_slot).astype(jnp.float32)


def attend(queries, projected_key_rows, projected_value_rows, labels):
    total_rows = queries.shape[0]
    kv_heads = projected_key_rows.shape[1]
    queries = queries.reshape(total_rows, kv_heads, -1, queries.shape[-1])
    scores = jnp.einsum(
        "qcgd,kcd->cgqk", queries, projected_key_rows, preferred_element_type=jnp.float32
    )
    scores = scores / jnp.sqrt(jnp.float32(queries.shape[-1]))
    index = jnp.arange(total_rows, dtype=jnp.int32)
    seen = (
        (labels[:, None] == labels[None, :])
        & (labels[:, None] >= 0)
        & (index[None, :] <= index[:, None])
    )
    seen = seen | (index[:, None] == index[None, :])
    scores = jnp.where(seen, scores, -1e30)
    largest = jnp.max(scores, axis=-1, keepdims=True)
    expo = jnp.where(seen, jnp.exp(scores - largest), 0.0)
    denominator = jnp.sum(expo, axis=-1, keepdims=True)
    probs = expo.astype(jnp.bfloat16)
    summed = jnp.einsum(
        "cgqk,kcd->qcgd", probs, projected_value_rows, preferred_element_type=jnp.float32
    )
    summed = summed / jnp.transpose(denominator, (2, 0, 1, 3))
    living = (labels >= 0).astype(jnp.float32)
    return (summed.reshape(total_rows, -1) * living[:, None]).astype(jnp.bfloat16)


def local(hidden, segment_ids, w_query, key_matrix, value_matrix):
    outboxes = hidden.shape[1]
    arrivals = [(hidden[:, 0], segment_ids[:, 0])]
    for stride in range(1, outboxes):
        arrivals.append(shifted((hidden[:, stride], segment_ids[:, stride]), "dp", stride))
    tokens_in = jnp.stack([entry[0] for entry in arrivals], axis=1)
    segments = jnp.stack([entry[1] for entry in arrivals], axis=1)
    where_all = positions(segments)
    box_ids = jnp.arange(outboxes, dtype=jnp.int32)[None, :, None]
    labels = jnp.where(segments >= 0, box_ids * NSEG + segments, -1).reshape(-1)
    query_cols = w_query.shape[1]
    key_cols = key_matrix.shape[1]
    w_joined = jnp.concatenate([w_query, key_matrix, value_matrix], axis=1)
    portion = lax.all_gather(tokens_in, "sp", axis=2, tiled=True)
    width_rows = portion.shape[2]
    flat = portion.reshape(-1, portion.shape[3])
    product = jnp.dot(flat, w_joined, preferred_element_type=jnp.float32)
    where_part = where_all.reshape(-1)
    queries = rotate(
        product[:, :query_cols].reshape(flat.shape[0], -1, HEAD_SIZE), where_part
    ).astype(jnp.bfloat16)
    projected_key_rows = rotate(
        product[:, query_cols : query_cols + key_cols].reshape(flat.shape[0], -1, HEAD_SIZE),
        where_part,
    ).astype(jnp.bfloat16)
    projected_value_rows = product[:, query_cols + key_cols :].astype(jnp.bfloat16)
    joined = jnp.concatenate(
        [
            queries.reshape(flat.shape[0], -1),
            projected_key_rows.reshape(flat.shape[0], -1),
            projected_value_rows,
        ],
        axis=1,
    )
    projected = joined.reshape(1, outboxes, width_rows, -1)
    projected = projected.reshape(GROUP_SLOTS, -1)
    queries = projected[:, :query_cols].reshape(GROUP_SLOTS, -1, HEAD_SIZE)
    projected_key_rows = projected[:, query_cols : query_cols + key_cols].reshape(
        GROUP_SLOTS, -1, HEAD_SIZE
    )
    projected_value_rows = projected[:, query_cols + key_cols :].reshape(GROUP_SLOTS, -1, HEAD_SIZE)
    attended = attend(queries, projected_key_rows, projected_value_rows, labels).reshape(
        1, GROUP_SLOTS, -1
    )
    return lax.all_to_all(attended, "sp", split_axis=1, concat_axis=2, tiled=True)


def solution(mesh):
    placed = (
        P("dp", None, "sp", None),
        P("dp", None, None),
        P(None, "sp"),
        P(None, "sp"),
        P(None, "sp"),
    )
    return jax.shard_map(
        local, mesh=mesh, in_specs=placed, out_specs=P("dp", "sp", None), check_vma=False
    )
```

profile of v0, /device:TPU:6, one launch (start us, length us, event | category | flops | bytes accessed | tf_op | source)
XLA Modules:
  0.0 151.7 jit_solution(342292011334748495)
XLA Ops:
  8.0 1.9 %collective-permute-start = (bf16[1,32,3584]{2,1,0:T(8,128)(2,1)S(1)}, bf16[1,32,3584]{2,1,0:T(8,128)(2,1)S(1)}, u32[]{:S(2)}, u32[]{:S(2)}) collective-permute-start(bf16[1,32,3584]{2,1,0:T(8,128)(2,1)S(1)} %get-tuple-element.13), channel_id=1, source_target_pairs={{0,4},{4,8},{8,12},{12,16},{16,20},{20,24},{24,28},{28,32},{32,36}... | collective-permute-start | bytes 688136 | tf_op jit(solution)/shard_map/ppermute | solution.py:17
  9.9 4.3 %collective-permute-start.1 = (bf16[1,32,3584]{2,1,0:T(8,128)(2,1)S(1)}, bf16[1,32,3584]{2,1,0:T(8,128)(2,1)S(1)}, u32[]{:S(2)}, u32[]{:S(2)}) collective-permute-start(bf16[1,32,3584]{2,1,0:T(8,128)(2,1)S(1)} %get-tuple-element.15), channel_id=1, source_target_pairs={{0,8},{4,12},{8,16},{12,20},{16,24},{20,28},{24,32},{28,36},{32,40... | collective-permute-start | bytes 688136 | tf_op jit(solution)/shard_map/ppermute | solution.py:17
  14.2 6.1 %collective-permute-start.2 = (bf16[1,32,3584]{2,1,0:T(8,128)(2,1)S(1)}, bf16[1,32,3584]{2,1,0:T(8,128)(2,1)S(1)}, u32[]{:S(2)}, u32[]{:S(2)}) collective-permute-start(bf16[1,32,3584]{2,1,0:T(8,128)(2,1)S(1)} %get-tuple-element.14), channel_id=1, source_target_pairs={{0,12},{4,16},{8,20},{12,24},{16,28},{20,32},{24,36},{28,40},{32,4... | collective-permute-start | bytes 688136 | tf_op jit(solution)/shard_map/ppermute | solution.py:17
  20.3 8.3 %collective-permute-done = bf16[1,32,3584]{2,1,0:T(8,128)(2,1)S(1)} collective-permute-done((bf16[1,32,3584]{2,1,0:T(8,128)(2,1)S(1)}, bf16[1,32,3584]{2,1,0:T(8,128)(2,1)S(1)}, u32[]{:S(2)}, u32[]{:S(2)}) %collective-permute-start) | collective-permute-done | bytes 229408 | tf_op jit(solution)/shard_map/ppermute | solution.py:17
  28.6 5.2 %collective-permute-done.1 = bf16[1,32,3584]{2,1,0:T(8,128)(2,1)S(1)} collective-permute-done((bf16[1,32,3584]{2,1,0:T(8,128)(2,1)S(1)}, bf16[1,32,3584]{2,1,0:T(8,128)(2,1)S(1)}, u32[]{:S(2)}, u32[]{:S(2)}) %collective-permute-start.1) | collective-permute-done | bytes 229408 | tf_op jit(solution)/shard_map/ppermute | solution.py:17
  33.9 8.0 %collective-permute-done.2 = bf16[1,32,3584]{2,1,0:T(8,128)(2,1)S(1)} collective-permute-done((bf16[1,32,3584]{2,1,0:T(8,128)(2,1)S(1)}, bf16[1,32,3584]{2,1,0:T(8,128)(2,1)S(1)}, u32[]{:S(2)}, u32[]{:S(2)}) %collective-permute-start.2) | collective-permute-done | bytes 229408 | tf_op jit(solution)/shard_map/ppermute | solution.py:17
  43.0 1.9 %collective-permute-start.4 = (s32[1,128]{1,0:T(1,128)S(1)}, s32[1,128]{1,0:T(1,128)S(1)}, u32[]{:S(2)}, u32[]{:S(2)}) collective-permute-start(s32[1,128]{1,0:T(1,128)S(1)} %get-tuple-element.24), channel_id=1, source_target_pairs={{0,8},{4,12},{8,16},{12,20},{16,24},{20,28},{24,32},{28,36},{32,40... | collective-permute-start | bytes 1544 | tf_op jit(solution)/shard_map/ppermute | solution.py:17
  44.9 1.9 %collective-permute-start.5 = (s32[1,128]{1,0:T(1,128)S(1)}, s32[1,128]{1,0:T(1,128)S(1)}, u32[]{:S(2)}, u32[]{:S(2)}) collective-permute-start(s32[1,128]{1,0:T(1,128)S(1)} %get-tuple-element.23), channel_id=1, source_target_pairs={{0,12},{4,16},{8,20},{12,24},{16,28},{20,32},{24,36},{28,40},{32,4... | collective-permute-start | bytes 1544 | tf_op jit(solution)/shard_map/ppermute | solution.py:17
  46.9 1.9 %collective-permute-start.3 = (s32[1,128]{1,0:T(1,128)S(1)}, s32[1,128]{1,0:T(1,128)S(1)}, u32[]{:S(2)}, u32[]{:S(2)}) collective-permute-start(s32[1,128]{1,0:T(1,128)S(1)} %get-tuple-element.22), channel_id=1, source_target_pairs={{0,4},{4,8},{8,12},{12,16},{16,20},{20,24},{24,28},{28,32},{32,36}... | collective-permute-start | bytes 1544 | tf_op jit(solution)/shard_map/ppermute | solution.py:17
  48.8 3.0 %collective-permute-done.4 = s32[1,128]{1,0:T(1,128)S(1)} collective-permute-done((s32[1,128]{1,0:T(1,128)S(1)}, s32[1,128]{1,0:T(1,128)S(1)}, u32[]{:S(2)}, u32[]{:S(2)}) %collective-permute-start.4) | collective-permute-done | bytes 544 | tf_op jit(solution)/shard_map/ppermute | solution.py:17
  51.8 2.3 %collective-permute-done.5 = s32[1,128]{1,0:T(1,128)S(1)} collective-permute-done((s32[1,128]{1,0:T(1,128)S(1)}, s32[1,128]{1,0:T(1,128)S(1)}, u32[]{:S(2)}, u32[]{:S(2)}) %collective-permute-start.5) | collective-permute-done | bytes 544 | tf_op jit(solution)/shard_map/ppermute | solution.py:17
  55.7 1.8 %multiply_cosine_fusion = (f32[512,64]{1,0:T(8,128)S(1)}, f32[512,64]{1,0:T(8,128)}) fusion(f32[64]{0:T(128)S(1)} %negate_power_fusion, f32[512]{0:T(512)S(1)} %convert_bitcast_fusion), kind=kLoop, calls=%fused_computation.28 | loop fusion | flops 32768 | bytes 264448 | tf_op jit(solution)/shard_map/cos | solution.py:24
  57.5 28.2 %all-gather.2.cloned.1.call-done = bf16[1,4,128,3584]{3,2,1,0:T(8,128)(2,1)} async-done(((bf16[1,4,32,3584]{3,2,1,0:T(8,128)(2,1)}), bf16[1,4,128,3584]{3,2,1,0:T(8,128)(2,1)}) %all-gather.2.cloned.1.call-update) | async-done | bytes 3670032 | tf_op jit(solution)/shard_map/all_gather | solution.py:86
  85.7 8.8 %fusion = f32[512,1152]{1,0:T(8,128)S(1)} fusion(bf16[512,3584]{1,0:T(8,128)(2,1)} %bitcast.107, bf16[3584,128]{1,0:T(8,128)(2,1)S(1)} %copy-done.2, bf16[3584,128]{1,0:T(8,128)(2,1)S(1)} %copy-done.3, bf16[3584,896]{1,0:T(8,128)(2,1)} %param.7), kind=kOutput, calls=%fused_computation | convolution fusion | flops 4252631040 | bytes 14286848 | tf_op jit(solution)/shard_map/dot_general | solution.py:89
  96.5 1.8 %copy.55 = f32[512,896]{0,1:T(8,128)S(1)} copy(f32[512,896]{1,0:T(8,128)} %slice.65) | data formatting | bytes 3670016 | tf_op jit(solution)/shard_map/slice | solution.py:92
  99.4 1.7 %copy.68 = f32[512,7,64]{2,0,1:T(8,128)S(1)} copy(f32[512,7,64]{0,2,1:T(8,128)} %get-tuple-element.11) | data formatting | bytes 1835008
  101.2 1.8 %copy.69 = f32[512,7,64]{2,0,1:T(8,128)} copy(f32[512,7,64]{0,2,1:T(8,128)S(1)} %get-tuple-element.10) | data formatting | bytes 1835008
  104.1 2.0 %subtract_convert_fusion = (bf16[512,7,64]{2,0,1:T(8,128)(2,1)S(1)}, bf16[512,7,64]{2,0,1:T(8,128)(2,1)S(1)}) fusion(f32[512,7,64]{2,0,1:T(8,128)} %copy.69, f32[512,7,64]{2,0,1:T(8,128)S(1)} %copy.68, f32[512,64]{1,0:T(8,128)} %get-tuple-element.19, f32[512,64]{1,0:T(8,128)S(1)} %get-tuple-element.18), kind=kLoop, calls=%fused_computation.17 | loop fusion | flops 1835008 | bytes 3014656 | tf_op jit(solution)/shard_map/convert
  106.1 2.0 %fusion.6 = (f32[7,512]{1,0:T(8,128)S(1)}, f32[512,512,7]{1,0,2:T(8,128)S(1)}) fusion(pred[512,512]{0,1:T(8,128)(4,1)S(1)} %fusion.16, bf16[512,7,64]{2,0,1:T(8,128)(2,1)S(1)} %get-tuple-element.9, bf16[512,7,64]{2,0,1:T(8,128)(2,1)S(1)} %get-tuple-element.8, bf16[512,64]{1,0:T(8,128)(2,1)S(1)} %get-tuple-element.17, bf16[512,64]{1,0:T(8,128)(2,1)S(1)} %get-tuple-element.16), kind=kOutput, calls=%fused_computation.8 | convolution fusion | flops 477360640 | bytes 8665088 | tf_op jit(solution)/shard_map/qcgd,kcd->cgqk/dot_general | solution.py:49
  108.2 1.8 %fusion.7 = f32[7,512]{1,0:T(8,128)S(1)} fusion(f32[512,512,7]{1,0,2:T(8,128)S(1)} %get-tuple-element.26, f32[7,512]{1,0:T(8,128)S(1)} %get-tuple-element.25, pred[512,512]{0,1:T(8,128)(4,1)S(1)} %fusion.16), kind=kLoop, calls=%fused_computation.9 | loop fusion | flops 9171456 | bytes 7630848 | tf_op jit(solution)/shard_map/reduce_sum | solution.py:63
  109.9 4.6 %bitcast_divide_fusion = f32[512,1,7,128]{0,3,2,1:T(8,128)} fusion(f32[512,512,7]{1,0,2:T(8,128)S(1)} %get-tuple-element.26, f32[7,512]{1,0:T(8,128)S(1)} %get-tuple-element.25, pred[512,512]{0,1:T(8,128)(4,1)S(1)} %fusion.16, f32[512,7]{0,1:T(8,128)S(1)} %bitcast.99, f32[512,1152]{1,0:T(8,128)} %copy-done), kind=kOutput, calls=%fused_computation.14 | convolution fusion | flops 479395840 | bytes 9596928 | tf_op jit(solution)/shard_map/cgqk,kcd->qcgd/dot_general | solution.py:65
  114.5 1.8 %copy.60 = f32[1,512,896]{2,1,0:T(8,128)S(1)} copy(f32[1,512,896]{1,2,0:T(8,128)} %bitcast.95) | data formatting | bytes 3670016 | tf_op jit(solution)/shard_map/reshape | solution.py:70
  118.5 6.2 %reduce.4 = bf16[512,896]{1,0:T(8,128)(2,1)S(1)} reduce(bf16[512,1,896]{2,1,0:T(2,128)(2,1)S(1)} %bitcast.91, bf16[]{:T(256)} %broadcast.256), dimensions={1}, to_apply=%bitcast.89.reduce_sub_computation | reduce | bytes 1835010
  125.0 16.9 %all_to_all.18 = bf16[4,2,57344]{2,1,0:T(2,128)(2,1)S(1)} all-to-all(bf16[4,2,57344]{2,1,0:T(2,128)(2,1)S(1)} %reshape.393), channel_id=1, replica_groups=mesh['dp'=192,'sp'=4] {'sp'}, dimensions={0} | all-to-all | bytes 1835008 | tf_op jit(solution)/shard_map/all_to_all | solution.py:117
  (36 shorter events, 13.8 us)
Async XLA Ops:
  6.5 36.4 %copy-start.1 = (s32[1,4,128]{2,1,0:T(4,128)S(1)}, s32[1,4,128]{2,1,0:T(4,128)}, u32[]{:S(2)}) copy-start(s32[1,4,128]{2,1,0:T(4,128)} %param.6) | copy-start | bytes 6148
  6.5 79.1 %copy-start.3 = (bf16[3584,128]{1,0:T(8,128)(2,1)S(1)}, bf16[3584,128]{1,0:T(8,128)(2,1)}, u32[]{:S(2)}) copy-start(bf16[3584,128]{1,0:T(8,128)(2,1)} %param.8) | copy-start | bytes 2752516
  6.5 79.1 %copy-start.2 = (bf16[3584,128]{1,0:T(8,128)(2,1)S(1)}, bf16[3584,128]{1,0:T(8,128)(2,1)}, u32[]{:S(2)}) copy-start(bf16[3584,128]{1,0:T(8,128)(2,1)} %param.9) | copy-start | bytes 2752516
  6.5 79.1 %all-gather.2.cloned.1.call-start = ((), (), s32[]{:S(2)}) async-start(), calls=%async_computation.1 | async-start | bytes 4587520 | tf_op jit(solution)/shard_map/all_gather | solution.py:86
  8.0 20.6 %collective-permute-start = (bf16[1,32,3584]{2,1,0:T(8,128)(2,1)S(1)}, bf16[1,32,3584]{2,1,0:T(8,128)(2,1)S(1)}, u32[]{:S(2)}, u32[]{:S(2)}) collective-permute-start(bf16[1,32,3584]{2,1,0:T(8,128)(2,1)S(1)} %get-tuple-element.13), channel_id=1, source_target_pairs={{0,4},{4,8},{8,12},{12,16},{16,20},{20,24},{24,28},{28,32},{32,36}... | collective-permute-start | bytes 688136 | tf_op jit(solution)/shard_map/ppermute | solution.py:17
  9.9 23.9 %collective-permute-start.1 = (bf16[1,32,3584]{2,1,0:T(8,128)(2,1)S(1)}, bf16[1,32,3584]{2,1,0:T(8,128)(2,1)S(1)}, u32[]{:S(2)}, u32[]{:S(2)}) collective-permute-start(bf16[1,32,3584]{2,1,0:T(8,128)(2,1)S(1)} %get-tuple-element.15), channel_id=1, source_target_pairs={{0,8},{4,12},{8,16},{12,20},{16,24},{20,28},{24,32},{28,36},{32,40... | collective-permute-start | bytes 688136 | tf_op jit(solution)/shard_map/ppermute | solution.py:17
  14.2 27.7 %collective-permute-start.2 = (bf16[1,32,3584]{2,1,0:T(8,128)(2,1)S(1)}, bf16[1,32,3584]{2,1,0:T(8,128)(2,1)S(1)}, u32[]{:S(2)}, u32[]{:S(2)}) collective-permute-start(bf16[1,32,3584]{2,1,0:T(8,128)(2,1)S(1)} %get-tuple-element.14), channel_id=1, source_target_pairs={{0,12},{4,16},{8,20},{12,24},{16,28},{20,32},{24,36},{28,40},{32,4... | collective-permute-start | bytes 688136 | tf_op jit(solution)/shard_map/ppermute | solution.py:17
  43.0 8.8 %collective-permute-start.4 = (s32[1,128]{1,0:T(1,128)S(1)}, s32[1,128]{1,0:T(1,128)S(1)}, u32[]{:S(2)}, u32[]{:S(2)}) collective-permute-start(s32[1,128]{1,0:T(1,128)S(1)} %get-tuple-element.24), channel_id=1, source_target_pairs={{0,8},{4,12},{8,16},{12,20},{16,24},{20,28},{24,32},{28,36},{32,40... | collective-permute-start | bytes 1544 | tf_op jit(solution)/shard_map/ppermute | solution.py:17
  44.9 9.1 %collective-permute-start.5 = (s32[1,128]{1,0:T(1,128)S(1)}, s32[1,128]{1,0:T(1,128)S(1)}, u32[]{:S(2)}, u32[]{:S(2)}) collective-permute-start(s32[1,128]{1,0:T(1,128)S(1)} %get-tuple-element.23), channel_id=1, source_target_pairs={{0,12},{4,16},{8,20},{12,24},{16,28},{20,32},{24,36},{28,40},{32,4... | collective-permute-start | bytes 1544 | tf_op jit(solution)/shard_map/ppermute | solution.py:17
  46.9 8.2 %collective-permute-start.3 = (s32[1,128]{1,0:T(1,128)S(1)}, s32[1,128]{1,0:T(1,128)S(1)}, u32[]{:S(2)}, u32[]{:S(2)}) collective-permute-start(s32[1,128]{1,0:T(1,128)S(1)} %get-tuple-element.22), channel_id=1, source_target_pairs={{0,4},{4,8},{8,12},{12,16},{16,20},{20,24},{24,28},{28,32},{32,36}... | collective-permute-start | bytes 1544 | tf_op jit(solution)/shard_map/ppermute | solution.py:17
  94.5 2.0 %copy-start = (f32[512,1152]{1,0:T(8,128)}, f32[512,1152]{1,0:T(8,128)S(1)}, u32[]{:S(2)}) copy-start(f32[512,1152]{1,0:T(8,128)S(1)} %fusion) | copy-start | bytes 7077892
Sparse Core Ops, SparseCore 0:
  43.1 42.5 all-gather.1
where the time goes:
time: 154 us; the launch traced here: 152 us
  waiting for transfers between devices  56 us (36%)
  starting transfers between devices  18 us (12%)
  local copies, waits for them, and re-layouts  16.9 us (11%)
  blocking collectives  16.9 us (11%)
  matrix products  15.5 us (10%)
  other arithmetic  14.7 us (10%)
  between operations  13.6 us (9%)
    all_gather x1, waiting for transfers between devices, local(): portion = lax.all_gather(tokens_in, 'sp', axis=2, tiled=True)  28.2 us
    ppermute x6, waiting for transfers between devices, shifted(): return lax.ppermute(value, axis, pairs)  27.8 us
    ppermute x6, starting transfers between devices, shifted(): return lax.ppermute(value, axis, pairs)  18 us
    all_to_all x1, blocking collectives, local(): lax.all_to_all(attended, 'sp', split_axis=1, concat_axis=2, tiled=True)  16.9 us
    dot_general x1, matrix products, local(): product = jnp.dot(flat, w_joined, preferred_element_type=jnp.float32)  8.85 us
    unnamed x1, other arithmetic  6.23 us
    unnamed x14, local copies, waits for them, and re-layouts  5.78 us
    dot_general x1, matrix products, attend(): jnp.einsum('cgqk,kcd->qcgd', probs, projected_value_rows, preferred_eleme...  4.6 us
  transfers between devices with their start and end apart: 7, of which 7 were waited for; matrix products, arithmetic and copies ran while one was open for 2% of the time, Pallas kernels for 0%

commit v1 on v0

v1 whole, which is shorter than its diff:
```python
import functools
import math

import jax
import jax.numpy as jnp
from jax import lax
from jax.experimental import pallas as pl
from jax.experimental.pallas import tpu as pltpu
from jax.sharding import PartitionSpec as P

HEAD = 128
BOXES = 4
ROPE_BASE = 1000000.0
MESH = pl.DeviceIdType.MESH


def kernel(hidden, seg, w_query, key_matrix, value_matrix, freq, out,
           tok, segs, weights, cosine, sine, seen, alive, queries, keys, values, staged, relay,
           load_sem, shift_send, shift_recv, seg_send, seg_recv,
           own_send, own_recv, pass_send, pass_recv,
           give_send, give_recv, hop_send, hop_recv, end_send, end_recv):
    ndp = lax.axis_size("dp")
    nsp = lax.axis_size("sp")
    me_dp = lax.axis_index("dp")
    me = lax.axis_index("sp")
    core = lax.rem(me_dp, 2)
    right = lax.rem(me + 1, nsp)
    left = lax.rem(me + nsp - 1, nsp)
    across = lax.rem(me + 2, nsp)
    part = hidden.shape[2]
    half = part // 2
    rows = BOXES * part
    q_cols = w_query.shape[1]
    heads = q_cols // HEAD

    def box_of(step):
        return lax.select(core == 0, step, lax.rem(BOXES - step, BOXES))

    def slot(box, owner):
        return tok.at[box, pl.ds(pl.multiple_of(owner * part, part), part)]

    def slot_half(box, owner, which):
        return tok.at[box, pl.ds(pl.multiple_of(owner * part + which * half, half), half)]

    def remote(src, dst, send, recv, dp, sp):
        return pltpu.make_async_remote_copy(
            src_ref=src, dst_ref=dst, send_sem=send, recv_sem=recv,
            device_id=(dp, sp), device_id_type=MESH)

    loads = [
        pltpu.make_async_copy(hidden.at[0, 0], slot(0, me), load_sem.at[0]),
        pltpu.make_async_copy(seg.at[0], segs.at[0], load_sem.at[1]),
        pltpu.make_async_copy(key_matrix, weights.at[:, pl.ds(q_cols, HEAD)], load_sem.at[2]),
        pltpu.make_async_copy(value_matrix, weights.at[:, pl.ds(q_cols + HEAD, HEAD)], load_sem.at[3]),
        pltpu.make_async_copy(w_query, weights.at[:, pl.ds(0, q_cols)], load_sem.at[4]),
    ]
    for load in loads:
        load.start()

    barrier = pltpu.get_barrier_semaphore()
    for step in (1, 2, 3):
        pl.semaphore_signal(barrier, inc=1, device_id=(lax.rem(me_dp + step, ndp), me), device_id_type=MESH)
        pl.semaphore_signal(barrier, inc=1, device_id=(lax.rem(me_dp + ndp - step, ndp), me), device_id_type=MESH)
    for peer in (right, left, across):
        pl.semaphore_signal(barrier, inc=1, device_id=(me_dp, peer), device_id_type=MESH)
    pl.semaphore_wait(barrier, 9)

    def own_copy(src, box, direction, which):
        peer = right if direction == 0 else left
        return remote(src, slot_half(box, me, which), own_send.at[box, direction, which],
                      own_recv.at[box, direction, which], me_dp, peer)

    def own_start(box, source):
        for order in (0, 1):
            for direction in (0, 1):
                which = order if direction == 0 else 1 - order
                own_copy(source(which), box, direction, which).start()

    def pass_copy(box, direction):
        peer = right if direction == 0 else left
        origin = left if direction == 0 else right
        return remote(slot_half(box, origin, direction), slot_half(box, origin, direction),
                      pass_send.at[box, direction], pass_recv.at[box, direction], me_dp, peer)

    def own_wait(box, direction, which):
        origin = left if direction == 0 else right
        remote(slot_half(box, origin, which), slot_half(box, origin, which),
               own_send.at[box, direction, which], own_recv.at[box, direction, which],
               me_dp, right).wait_recv()

    def seg_copy(box):
        return remote(seg.at[0], segs.at[box], seg_send.at[box], seg_recv.at[box],
                      lax.rem(me_dp + box, ndp), me)

    def shift_copy(box):
        return remote(hidden.at[0, box], slot(box, me), shift_send.at[box], shift_recv.at[box],
                      lax.rem(me_dp + box, ndp), me)

    own_start(0, lambda which: hidden.at[0, 0, pl.ds(which * half, half)])
    for box in (1, 2, 3):
        seg_copy(box).start()
    for order in (1, 2, 3):
        shift_copy(lax.select(core == 0, BOXES - order, order)).start()

    def give_columns(origin):
        return pl.ds(pl.multiple_of(origin * q_cols, HEAD), q_cols)

    def give_right(box):
        return remote(staged.at[box], out.at[0, :, give_columns(me)], give_send.at[0],
                      give_recv.at[0], me_dp, right)

    def give_left(box):
        return remote(staged.at[box], out.at[0, :, give_columns(me)], give_send.at[1],
                      give_recv.at[1], me_dp, left)

    def hop(box, direction):
        peer = right if direction == 0 else left
        return remote(staged.at[box, pl.ds(direction * (rows // 2), rows // 2)], relay.at[direction],
                      hop_send.at[direction], hop_recv.at[direction], me_dp, peer)

    def end_hop(direction):
        peer = right if direction == 0 else left
        origin = left if direction == 0 else right
        return remote(relay.at[direction],
                      out.at[0, pl.ds(direction * (rows // 2), rows // 2), give_columns(origin)],
                      end_send.at[direction], end_recv.at[direction], me_dp, peer)

    def keep(box):
        return pltpu.make_async_copy(staged.at[box], out.at[0, :, give_columns(me)], load_sem.at[5])

    def give(box):
        delta = lax.rem(box + nsp - me, nsp)

        @pl.when(delta == 0)
        def _():
            keep(box).start()

        @pl.when(delta == 1)
        def _():
            give_right(box).start()

        @pl.when(delta == 3)
        def _():
            give_left(box).start()

        @pl.when(delta == 2)
        def _():
            hop(box, 0).start()
            hop(box, 1).start()

    scale = 1.0 / math.sqrt(HEAD)
    row_id = lax.broadcasted_iota(jnp.int32, (rows, rows), 0)
    col_id = lax.broadcasted_iota(jnp.int32, (rows, rows), 1)

    def body(step, carry):
        box = box_of(step)
        for direction in (0, 1):
            own_wait(box, direction, direction)
            pass_copy(box, direction).start()

        @pl.when(step < BOXES - 1)
        def _():
            later = box_of(step + 1)
            shift_copy(later).wait_recv()
            own_start(later, lambda which: slot_half(later, me, which))

        @pl.when(step == BOXES - 1)
        def _():
            for before in range(BOXES - 1):
                give(box_of(before))

        @pl.when(step == 0)
        def _():
            loads[1].wait()

        @pl.when(step > 0)
        def _():
            seg_copy(box).wait_recv()

        seg_row = jnp.broadcast_to(segs[box, pl.ds(box, 1), :], (rows, rows))
        seg_col = jnp.transpose(seg_row)
        below = jnp.where((seg_row >= 0) & (seg_row < seg_col), 1.0, 0.0)
        first = jnp.sum(below, axis=1, keepdims=True)
        where = row_id.astype(jnp.float32) - first
        angle = where * freq[0:1, :]
        cosine[...] = jnp.cos(angle)
        swing = jnp.sin(angle)
        sine[...] = jnp.where(col_id < HEAD // 2, -swing, swing)
        same = (seg_row == seg_col) & (seg_col >= 0) & (col_id <= row_id)
        seen[...] = jnp.where(same | (col_id == row_id), 0.0, -1e30)
        alive[...] = jnp.where(seg_col >= 0, 1.0, 0.0)

        @pl.when(step == 0)
        def _():
            for load in (loads[0], loads[2], loads[3], loads[4]):
                load.wait()

        for direction in (0, 1):
            own_wait(box, direction, 1 - direction)
            pass_copy_wait = remote(
                slot_half(box, across, direction), slot_half(box, across, direction),
                pass_send.at[box, direction], pass_recv.at[box, direction], me_dp, right)
            pass_copy_wait.wait_recv()

        def turned(value):
            return value * cosine[...] + pltpu.roll(value, HEAD // 2, 1) * sine[...]

        both = jnp.dot(tok[box], weights[:, q_cols:], preferred_element_type=jnp.float32)
        keys[...] = turned(both[:, :HEAD]).astype(jnp.bfloat16)
        values[...] = both[:, HEAD:].astype(jnp.bfloat16)
        for begin in range(0, heads, 2):
            count = min(2, heads - begin)
            product = jnp.dot(tok[box], weights[:, begin * HEAD:(begin + count) * HEAD],
                              preferred_element_type=jnp.float32)
            for index in range(count):
                query = turned(product[:, index * HEAD:(index + 1) * HEAD])
                queries[begin + index] = query.astype(jnp.bfloat16)
        for index in range(heads):
            scores = lax.dot_general(queries[index], keys[...], (((1,), (1,)), ((), ())),
                                     preferred_element_type=jnp.float32) * scale
            scores = jnp.where(seen[...] == 0.0, scores, -1e30)
            top = jnp.max(scores, axis=1, keepdims=True)
            expo = jnp.exp(scores - top)
            total = jnp.sum(expo, axis=1, keepdims=True)
            mixed = jnp.dot(expo.astype(jnp.bfloat16), values[...], preferred_element_type=jnp.float32)
            mixed = mixed * (alive[...] / total)
            staged[box, :, index * HEAD:(index + 1) * HEAD] = mixed.astype(jnp.bfloat16)

        @pl.when(step == BOXES - 1)
        def _():
            give(box)
        return carry

    lax.fori_loop(0, BOXES, body, 0)

    for direction in (0, 1):
        hop(0, direction).wait_recv()
        end_hop(direction).start()
    give_right(0).wait()
    give_left(0).wait()
    keep(0).wait()
    for direction in (0, 1):
        hop(0, direction).wait_send()
        end_hop(direction).wait()
    for box in (1, 2, 3):
        seg_copy(box).wait_send()
        shift_copy(box).wait_send()
    for box in range(BOXES):
        for direction in (0, 1):
            pass_copy(box, direction).wait_send()
            for which in (0, 1):
                own_copy(slot_half(box, me, which), box, direction, which).wait_send()


def local(hidden, segment_ids, w_query, key_matrix, value_matrix):
    depth = hidden.shape[3]
    part = hidden.shape[2]
    rows = BOXES * part
    q_cols = w_query.shape[1]
    width = q_cols + 2 * HEAD
    heads = q_cols // HEAD
    freq = ROPE_BASE ** (-(jnp.arange(HEAD // 2, dtype=jnp.float32) * 2.0 / HEAD))
    freq = jnp.broadcast_to(jnp.concatenate([freq, freq])[None, :], (8, HEAD))
    dma = pltpu.SemaphoreType.DMA
    flops = 2 * BOXES * rows * depth * width
    return pl.pallas_call(
        kernel,
        out_shape=jax.ShapeDtypeStruct((1, rows, 4 * q_cols), jnp.bfloat16),
        in_specs=[pl.BlockSpec(memory_space=pltpu.HBM)] * 5 + [pl.BlockSpec(memory_space=pltpu.VMEM)],
        out_specs=pl.BlockSpec(memory_space=pltpu.HBM),
        scratch_shapes=[
            pltpu.VMEM((BOXES, rows, depth), jnp.bfloat16),
            pltpu.VMEM((BOXES, BOXES, rows), jnp.int32),
            pltpu.VMEM((depth, width), jnp.bfloat16),
            pltpu.VMEM((rows, HEAD), jnp.float32),
            pltpu.VMEM((rows, HEAD), jnp.float32),
            pltpu.VMEM((rows, rows), jnp.float32),
            pltpu.VMEM((rows, HEAD), jnp.float32),
            pltpu.VMEM((heads, rows, HEAD), jnp.bfloat16),
            pltpu.VMEM((rows, HEAD), jnp.bfloat16),
            pltpu.VMEM((rows, HEAD), jnp.bfloat16),
            pltpu.VMEM((BOXES, rows, q_cols), jnp.bfloat16),
            pltpu.VMEM((2, rows // 2, q_cols), jnp.bfloat16),
            dma((6,)),
            dma((BOXES,)), dma((BOXES,)),
            dma((BOXES,)), dma((BOXES,)),
            dma((BOXES, 2, 2)), dma((BOXES, 2, 2)),
            dma((BOXES, 2)), dma((BOXES, 2)),
            dma((2,)), dma((2,)),
            dma((2,)), dma((2,)),
            dma((2,)), dma((2,)),
        ],
        compiler_params=pltpu.CompilerParams(
            collective_id=0, has_side_effects=True, vmem_limit_bytes=40 * 1024 * 1024),
        cost_estimate=pl.CostEstimate(flops=flops, bytes_accessed=12000000, transcendentals=0),
        name="fused_boxes",
    )(hidden, segment_ids, w_query, key_matrix, value_matrix, freq)


def solution(mesh):
    placed = (
        P("dp", None, "sp", None),
        P("dp", None, None),
        P(None, "sp"),
        P(None, "sp"),
        P(None, "sp"),
    )
    return jax.shard_map(
        local, mesh=mesh, in_specs=placed, out_specs=P("dp", "sp", None), check_vma=False
    )
```

time: 154 us -> 72.4 us (0.47); the launches traced: 152 us -> 72.1 us
  Pallas kernels: 0 us -> 64.1 us
  waiting for transfers between devices: 56 us -> 0 us
  starting transfers between devices: 18 us -> 0 us
  blocking collectives: 16.9 us -> 0 us
  matrix products: 15.5 us -> 0 us
  other arithmetic: 14.7 us -> 0.09 us
  between operations: 13.6 us -> 0.02 us
  local copies, waits for them, and re-layouts: 16.9 us -> 7.97 us
    pallas_call x0 -> x1, Pallas kernels: none -> 64.1 us  [local(): pl.pallas_call(kernel, out_shape=jax.ShapeDtypeStruct((1, rows, 4 * q_col...]
    all_gather x1 -> x0, waiting for transfers between devices: 28.2 us -> none  [local(): portion = lax.all_gather(tokens_in, 'sp', axis=2, tiled=True)]
    ppermute x6 -> x0, waiting for transfers between devices: 27.8 us -> none  [shifted(): return lax.ppermute(value, axis, pairs)]
    ppermute x6 -> x0, starting transfers between devices: 18 us -> none  [shifted(): return lax.ppermute(value, axis, pairs)]
    all_to_all x1 -> x0, blocking collectives: 16.9 us -> none  [local(): lax.all_to_all(attended, 'sp', split_axis=1, concat_axis=2, tiled=True)]
    dot_general x3 -> x0, matrix products: 15.5 us -> none  [the longest x1 8.85 us: local(): product = jnp.dot(flat, w_joined, preferred_element_type=jnp.float32)]
    unnamed x1 -> x0, other arithmetic: 6.23 us -> none
    slice x5 -> x0, local copies, waits for them, and re-layouts: 5.87 us -> none  [the longest x2 3.26 us: local(): product[:, :query_cols].reshape(flat.shape[0], -1, HEAD_SIZE)]
  transfers between devices with their start and end apart: 7 -> 0, of which waited for: 7 -> 0; matrix products, arithmetic and copies ran while one was open for 2% -> 0% of each run, Pallas kernels for 0% -> 0%
where the time goes in v1:
time: 72.4 us; the launch traced here: 72.1 us
  Pallas kernels  64.1 us (89%)
  local copies, waits for them, and re-layouts  7.97 us (11%)
    pallas_call x1, Pallas kernels, local(): pl.pallas_call(kernel, out_shape=jax.ShapeDtypeStruct((1, rows, 4 * q_col...  64.1 us
    unnamed x11, local copies, waits for them, and re-layouts  7.97 us

profile of v1, /device:TPU:6, one launch (start us, length us, event | category | flops | bytes accessed | tf_op | source)
XLA Modules:
  0.0 72.1 jit_solution(10536810010761866141)
XLA Ops:
  0.0 0.1 pad_maximum_fusion
  0.1 0.0 copy-start
  0.1 2.8 %copy-done = bf16[3584,896]{1,0:T(8,128)(2,1)S(1)} copy-done((bf16[3584,896]{1,0:T(8,128)(2,1)S(1)}, bf16[3584,896]{1,0:T(8,128)(2,1)}, u32[]{:S(2)}) %copy-start) | copy-done | bytes 6422552
  2.9 0.0 copy-start.1
  2.9 1.2 %copy-done.1 = bf16[1,4,32,3584]{3,2,1,0:T(8,128)(2,1)S(1)} copy-done((bf16[1,4,32,3584]{3,2,1,0:T(8,128)(2,1)S(1)}, bf16[1,4,32,3584]{3,2,1,0:T(8,128)(2,1)}, u32[]{:S(2)}) %copy-start.1) | copy-done | bytes 917528
  4.1 0.0 copy-start.2
  4.1 1.2 %copy-done.2 = bf16[3584,128]{1,0:T(8,128)(2,1)S(1)} copy-done((bf16[3584,128]{1,0:T(8,128)(2,1)S(1)}, bf16[3584,128]{1,0:T(8,128)(2,1)}, u32[]{:S(2)}) %copy-start.2) | copy-done | bytes 917528
  5.3 0.0 copy-start.3
  5.3 1.2 %copy-done.3 = bf16[3584,128]{1,0:T(8,128)(2,1)S(1)} copy-done((bf16[3584,128]{1,0:T(8,128)(2,1)S(1)}, bf16[3584,128]{1,0:T(8,128)(2,1)}, u32[]{:S(2)}) %copy-start.3) | copy-done | bytes 917528
  6.5 0.0 copy-start.4
  6.5 0.7 copy-done.4
  7.1 64.1 %fused_boxes.1 = bf16[1,128,3584]{2,1,0:T(8,128)(2,1)S(1)} custom-call(bf16[1,4,32,3584]{3,2,1,0:T(8,128)(2,1)S(1)} %copy-done.1, s32[1,4,128]{2,1,0:T(4,128)S(1)} %copy-done.4, bf16[3584,896]{1,0:T(8,128)(2,1)S(1)} %copy-done, bf16[3584,128]{1,0:T(8,128)(2,1)S(1)} %copy-done.2, bf16[3584,128]{1,0:T(8,128)(2,1)S(1)} %copy-done.3, ...), custom_call_target="tpu_custom_call" | custom-call | flops 4227858432 | bytes 12000000 | tf_op jit(solution)/shard_map/fused_boxes/pallas_call | solution.py:266
  71.2 0.9 %copy.7 = bf16[1,128,3584]{2,1,0:T(8,128)(2,1)} copy(bf16[1,128,3584]{2,1,0:T(8,128)(2,1)S(1)} %fused_boxes.1) | data formatting | bytes 1835008
  (2 shorter events, 0.0 us)
Async XLA Ops:
  0.1 2.8 %copy-start = (bf16[3584,896]{1,0:T(8,128)(2,1)S(1)}, bf16[3584,896]{1,0:T(8,128)(2,1)}, u32[]{:S(2)}) copy-start(bf16[3584,896]{1,0:T(8,128)(2,1)} %w_query.1) | copy-start | bytes 19267588
  2.9 1.2 %copy-start.1 = (bf16[1,4,32,3584]{3,2,1,0:T(8,128)(2,1)S(1)}, bf16[1,4,32,3584]{3,2,1,0:T(8,128)(2,1)}, u32[]{:S(2)}) copy-start(bf16[1,4,32,3584]{3,2,1,0:T(8,128)(2,1)} %hidden.1) | copy-start | bytes 2752516
  4.1 1.2 %copy-start.2 = (bf16[3584,128]{1,0:T(8,128)(2,1)S(1)}, bf16[3584,128]{1,0:T(8,128)(2,1)}, u32[]{:S(2)}) copy-start(bf16[3584,128]{1,0:T(8,128)(2,1)} %key_matrix.1) | copy-start | bytes 2752516
  5.3 1.2 %copy-start.3 = (bf16[3584,128]{1,0:T(8,128)(2,1)S(1)}, bf16[3584,128]{1,0:T(8,128)(2,1)}, u32[]{:S(2)}) copy-start(bf16[3584,128]{1,0:T(8,128)(2,1)} %value_matrix.1) | copy-start | bytes 2752516
  6.5 0.7 copy-start.4

commit v2 on v1

v2 whole, which is shorter than its diff:
```python
import functools
import math

import jax
import jax.numpy as jnp
from jax import lax
from jax.experimental import pallas as pl
from jax.experimental.pallas import tpu as pltpu
from jax.sharding import PartitionSpec as P

HEAD = 128
BOXES = 4
ROPE_BASE = 1000000.0
Z_CHIPS = 12
VMEM_LIMIT = 55300000
MESH = pl.DeviceIdType.MESH


def kernel(hidden, seg, w_query, key_matrix, value_matrix, out,
           tok, segs, weights, cosine, sine, seen, alive, queries, keys, values, staged, mine,
           load_sem, shift_send, shift_recv, seg_send, seg_recv,
           own_send, own_recv, pass_send, pass_recv, give_send, give_recv):
    ndp = lax.axis_size("dp")
    nsp = lax.axis_size("sp")
    me_dp = lax.axis_index("dp")
    me = lax.axis_index("sp")
    core = lax.rem(me_dp, 2)
    first_plane = lax.rem(lax.div(me_dp, 2), Z_CHIPS) == 0
    right = lax.rem(me + 1, nsp)
    left = lax.rem(me + nsp - 1, nsp)
    across = lax.rem(me + 2, nsp)
    part = hidden.shape[2]
    half = part // 2
    rows = BOXES * part
    q_cols = w_query.shape[1]
    heads = q_cols // HEAD

    def box_of(step):
        return lax.select((core == 1) & (step >= 2), 5 - step, step)

    def slot(box, owner):
        return tok.at[box, pl.ds(pl.multiple_of(owner * part, part), part)]

    def slot_half(box, owner, which):
        return tok.at[box, pl.ds(pl.multiple_of(owner * part + which * half, half), half)]

    def remote(src, dst, send, recv, dp, sp):
        return pltpu.make_async_remote_copy(
            src_ref=src, dst_ref=dst, send_sem=send, recv_sem=recv,
            device_id=(dp, sp), device_id_type=MESH)

    barrier = pltpu.get_barrier_semaphore()
    for peer in (right, left, across):
        pl.semaphore_signal(barrier, inc=1, device_id=(me_dp, peer), device_id_type=MESH)
    for box in (1, 2, 3):
        pl.semaphore_signal(barrier, inc=1, device_id=(lax.rem(me_dp + ndp - box, ndp), me), device_id_type=MESH)

    loads = [
        pltpu.make_async_copy(hidden.at[0, 0], slot(0, me), load_sem.at[0]),
        pltpu.make_async_copy(hidden.at[0, pl.ds(1, BOXES - 1)], mine, load_sem.at[1]),
        pltpu.make_async_copy(seg.at[0], segs.at[0], load_sem.at[5]),
        pltpu.make_async_copy(key_matrix, weights.at[:, pl.ds(q_cols, HEAD)], load_sem.at[2]),
        pltpu.make_async_copy(value_matrix, weights.at[:, pl.ds(q_cols + HEAD, HEAD)], load_sem.at[3]),
        pltpu.make_async_copy(w_query, weights.at[:, pl.ds(0, q_cols)], load_sem.at[4]),
    ]
    for load in loads:
        load.start()
    pl.semaphore_wait(barrier, 6)
    loads[0].wait()
    loads[1].wait()

    def own_copy(box, direction, which):
        peer = right if direction == 0 else left
        return remote(slot_half(box, me, which), slot_half(box, me, which), own_send.at[box, direction, which],
                      own_recv.at[box, direction, which], me_dp, peer)

    def own_start(box):
        for order in (0, 1):
            for direction in (0, 1):
                which = order if direction == 0 else 1 - order
                own_copy(box, direction, which).start()

    def pass_copy(box, direction):
        peer = right if direction == 0 else left
        origin = left if direction == 0 else right
        return remote(slot_half(box, origin, direction), slot_half(box, origin, direction),
                      pass_send.at[box, direction], pass_recv.at[box, direction], me_dp, peer)

    def own_wait(box, direction, which):
        origin = left if direction == 0 else right
        remote(slot_half(box, origin, which), slot_half(box, origin, which),
               own_send.at[box, direction, which], own_recv.at[box, direction, which],
               me_dp, right).wait_recv()

    def pass_wait(box, direction):
        remote(slot_half(box, across, direction), slot_half(box, across, direction),
               pass_send.at[box, direction], pass_recv.at[box, direction], me_dp, right).wait_recv()

    def seg_copy(box):
        return remote(segs.at[0], segs.at[box], seg_send.at[box], seg_recv.at[box],
                      lax.rem(me_dp + box, ndp), me)

    def shift_copy(box):
        return remote(mine.at[box - 1], slot(box, me), shift_send.at[box], shift_recv.at[box],
                      lax.rem(me_dp + box, ndp), me)

    def spread(step):
        shift_copy(box_of(step)).wait_recv()
        own_start(box_of(step))

    def forward(step):
        for direction in (0, 1):
            own_wait(box_of(step), direction, direction)
            pass_copy(box_of(step), direction).start()

    own_start(0)
    shift_copy(1).start()
    loads[2].wait()
    for box in (1, 2, 3):
        seg_copy(box).start()
    for box in (2, 3):
        shift_copy(box).start()
    forward(0)

    @pl.when(jnp.logical_not(first_plane & (core == 0)))
    def _():
        spread(1)

    def give_columns(origin):
        return pl.ds(pl.multiple_of(origin * q_cols, HEAD), q_cols)

    def give_copy(box, origin, delta):
        return remote(staged.at[box], out.at[0, :, give_columns(origin)], give_send.at[delta],
                      give_recv.at[origin], me_dp, box)

    def keep(box):
        return pltpu.make_async_copy(staged.at[box], out.at[0, :, give_columns(me)], load_sem.at[6])

    def give(box):
        delta = lax.rem(box + nsp - me, nsp)

        @pl.when(delta == 0)
        def _():
            keep(box).start()

        @pl.when(delta != 0)
        def _():
            give_copy(box, me, delta).start()

    scale = 1.0 / math.sqrt(HEAD)
    row_id = lax.broadcasted_iota(jnp.int32, (rows, rows), 0)
    col_id = lax.broadcasted_iota(jnp.int32, (rows, rows), 1)

    def body(step, carry):
        box = box_of(step)
        held = first_plane & (step == core)

        @pl.when((step < BOXES - 1) & jnp.logical_not(held))
        def _():
            forward(step + 1)

        @pl.when((step < BOXES - 2) & jnp.logical_not(first_plane & (step <= core)))
        def _():
            spread(step + 2)

        @pl.when(step > 0)
        def _():
            seg_copy(box).wait_recv()

        seg_row = jnp.broadcast_to(segs[box, pl.ds(box, 1), :], (rows, rows))
        seg_col = jnp.transpose(seg_row)
        below = jnp.where((seg_row >= 0) & (seg_row < seg_col), 1.0, 0.0)
        first = jnp.sum(below, axis=1, keepdims=True)
        where = row_id.astype(jnp.float32) - first
        lane = lax.rem(col_id, HEAD // 2).astype(jnp.float32)
        freq = jnp.exp(lane * (-2.0 * math.log(ROPE_BASE) / HEAD))
        angle = where * freq
        cosine[...] = jnp.cos(angle)
        swing = jnp.sin(angle)
        sine[...] = jnp.where(col_id < HEAD // 2, -swing, swing)
        same = (seg_row == seg_col) & (seg_col >= 0) & (col_id <= row_id)
        seen[...] = jnp.where(same | (col_id == row_id), 0.0, -1e30)
        alive[...] = jnp.where(seg_col >= 0, 1.0, 0.0)

        @pl.when(step == 0)
        def _():
            for load in loads[3:]:
                load.wait()

        for direction in (0, 1):
            own_wait(box, direction, 1 - direction)
            pass_wait(box, direction)

        @pl.when(step == BOXES - 1)
        def _():
            give(box_of(2))
            give(box_of(1))

            @pl.when(jnp.logical_not(first_plane & (core == 0)))
            def _():
                give(box_of(0))

        def turned(value):
            return value * cosine[...] + pltpu.roll(value, HEAD // 2, 1) * sine[...]

        both = jnp.dot(tok[box], weights[:, q_cols:], preferred_element_type=jnp.float32)
        keys[...] = turned(both[:, :HEAD]).astype(jnp.bfloat16)
        values[...] = both[:, HEAD:].astype(jnp.bfloat16)
        for begin in range(0, heads, 2):
            count = min(2, heads - begin)
            product = jnp.dot(tok[box], weights[:, begin * HEAD:(begin + count) * HEAD],
                              preferred_element_type=jnp.float32)
            for index in range(count):
                query = turned(product[:, index * HEAD:(index + 1) * HEAD])
                queries[begin + index] = query.astype(jnp.bfloat16)
        for index in range(heads):
            scores = lax.dot_general(queries[index], keys[...], (((1,), (1,)), ((), ())),
                                     preferred_element_type=jnp.float32) * scale
            scores = jnp.where(seen[...] == 0.0, scores, -1e30)
            top = jnp.max(scores, axis=1, keepdims=True)
            expo = jnp.exp(scores - top)
            total = jnp.sum(expo, axis=1, keepdims=True)
            mixed = jnp.dot(expo.astype(jnp.bfloat16), values[...], preferred_element_type=jnp.float32)
            mixed = mixed * (alive[...] / total)
            staged[box, :, index * HEAD:(index + 1) * HEAD] = mixed.astype(jnp.bfloat16)

        @pl.when((step == BOXES - 1) | (first_plane & (core == 0) & (step == 0)))
        def _():
            give(box)

        @pl.when(held)
        def _():
            spread(step + 1)
            forward(step + 1)
            spread(step + 2)
        return carry

    lax.fori_loop(0, BOXES, body, 0)

    for delta in (1, 2, 3):
        give_copy(0, lax.rem(me + delta, nsp), delta).wait_recv()
        give_copy(0, me, delta).wait_send()
    keep(0).wait()
    for box in (1, 2, 3):
        seg_copy(box).wait_send()
        shift_copy(box).wait_send()
    for box in range(BOXES):
        for direction in (0, 1):
            pass_copy(box, direction).wait_send()
            for which in (0, 1):
                own_copy(box, direction, which).wait_send()


def local(hidden, segment_ids, w_query, key_matrix, value_matrix):
    depth = hidden.shape[3]
    part = hidden.shape[2]
    rows = BOXES * part
    q_cols = w_query.shape[1]
    width = q_cols + 2 * HEAD
    heads = q_cols // HEAD
    dma = pltpu.SemaphoreType.DMA
    flops = 2 * BOXES * rows * depth * width
    return pl.pallas_call(
        kernel,
        out_shape=jax.ShapeDtypeStruct((1, rows, 4 * q_cols), jnp.bfloat16),
        in_specs=[pl.BlockSpec(memory_space=pltpu.HBM)] * 5,
        out_specs=pl.BlockSpec(memory_space=pltpu.HBM),
        scratch_shapes=[
            pltpu.VMEM((BOXES, rows, depth), jnp.bfloat16),
            pltpu.VMEM((BOXES, BOXES, rows), jnp.int32),
            pltpu.VMEM((depth, width), jnp.bfloat16),
            pltpu.VMEM((rows, HEAD), jnp.float32),
            pltpu.VMEM((rows, HEAD), jnp.float32),
            pltpu.VMEM((rows, rows), jnp.float32),
            pltpu.VMEM((rows, HEAD), jnp.float32),
            pltpu.VMEM((heads, rows, HEAD), jnp.bfloat16),
            pltpu.VMEM((rows, HEAD), jnp.bfloat16),
            pltpu.VMEM((rows, HEAD), jnp.bfloat16),
            pltpu.VMEM((BOXES, rows, q_cols), jnp.bfloat16),
            pltpu.VMEM((BOXES - 1, part, depth), jnp.bfloat16),
            dma((7,)),
            dma((BOXES,)), dma((BOXES,)),
            dma((BOXES,)), dma((BOXES,)),
            dma((BOXES, 2, 2)), dma((BOXES, 2, 2)),
            dma((BOXES, 2)), dma((BOXES, 2)),
            dma((BOXES,)), dma((BOXES,)),
        ],
        compiler_params=pltpu.CompilerParams(
            collective_id=0, has_side_effects=True, vmem_limit_bytes=VMEM_LIMIT),
        cost_estimate=pl.CostEstimate(flops=flops, bytes_accessed=12000000, transcendentals=0),
        name="fused_boxes",
    )(hidden, segment_ids, w_query, key_matrix, value_matrix)


def solution(mesh):
    placed = (
        P("dp", None, "sp", None),
        P("dp", None, None),
        P(None, "sp"),
        P(None, "sp"),
        P(None, "sp"),
    )
    return jax.shard_map(
        local, mesh=mesh, in_specs=placed, out_specs=P("dp", "sp", None), check_vma=False
    )
```

time: 72.4 us -> 65.8 us (0.909)
  the two profiles are of different devices: /device:TPU:6 before, /device:TPU:5 now
where the time goes in v2:
time: 65.8 us; the launch traced here: 65.6 us
  Pallas kernels  64 us (97%)
  local copies, waits for them, and re-layouts  1.61 us (2%)
    pallas_call x1, Pallas kernels, local(): pl.pallas_call(kernel, out_shape=jax.ShapeDtypeStruct((1, rows, 4 * q_col...  64 us
    unnamed x3, local copies, waits for them, and re-layouts  1.61 us

profile of v2, /device:TPU:5, one launch (start us, length us, event | category | flops | bytes accessed | tf_op | source)
XLA Modules:
  0.0 65.6 jit_solution(725732254511363765)
XLA Ops:
  0.0 0.0 copy-start
  0.0 0.7 %copy-done = s32[1,4,128]{2,1,0:T(4,128)S(1)} copy-done((s32[1,4,128]{2,1,0:T(4,128)S(1)}, s32[1,4,128]{2,1,0:T(4,128)}, u32[]{:S(2)}) %copy-start) | copy-done | bytes 2072
  0.7 64.0 %fused_boxes.1 = bf16[1,128,3584]{2,1,0:T(8,128)(2,1)S(1)} custom-call(bf16[1,4,32,3584]{3,2,1,0:T(8,128)(2,1)} %hidden.1, s32[1,4,128]{2,1,0:T(4,128)S(1)} %copy-done, bf16[3584,896]{1,0:T(8,128)(2,1)} %w_query.1, bf16[3584,128]{1,0:T(8,128)(2,1)} %key_matrix.1, bf16[3584,128]{1,0:T(8,128)(2,1)} %value_matrix.1), custom_call_target="tpu_custom_call" | custom-call | flops 4227858432 | bytes 12000000 | tf_op jit(solution)/shard_map/fused_boxes/pallas_call | solution.py:263
  64.7 0.9 %copy.7 = bf16[1,128,3584]{2,1,0:T(8,128)(2,1)} copy(bf16[1,128,3584]{2,1,0:T(8,128)(2,1)S(1)} %fused_boxes.1) | data formatting | bytes 1835008
Async XLA Ops:
  0.0 0.7 %copy-start = (s32[1,4,128]{2,1,0:T(4,128)S(1)}, s32[1,4,128]{2,1,0:T(4,128)}, u32[]{:S(2)}) copy-start(s32[1,4,128]{2,1,0:T(4,128)} %seg.1) | copy-start | bytes 6148
